TPU v7x, 32 devices: a whole 2x2x4 slice. The times are simulated.
32 devices in a mesh: var: 4 (over z), lat: 4 (over x, core), lon: 2 (over y).
Axes of the slice: x: 2, y: 2, z: 4, core: 2. Of those that a mesh axis runs over, the one named last changes fastest.
Arguments:
- state: bfloat16 [1, 256, 384, 1024], P(None, 'var', 'lat', 'lon'), may hold values from -6 to 6
- weights_in: bfloat16 [2, 256, 256], replicated, may hold values from -0.25 to 0.25
- bias_in: float32 [2, 256], replicated, may hold values from -3 to 3
- weights_out: bfloat16 [2, 256, 256], replicated, may hold values from -2 to 2
Outputs:
- field: bfloat16 [1, 256, 384, 1024], P(None, 'var', 'lat', 'lon')
- zonal: float32 [1, 256, 384], P(None, 'var', 'lat')
- energy: float32 [256], P('var')
All inputs are finite; a program needn't handle non-finite values.
Results may differ from a plain program's by a relative error of at most 0.012.
Values may be sent and summed in bfloat16 or wider, within the bound.
A program may use at most 64 MiB of HBM per device.

v0:
```python
import math
import jax
import jax.numpy as jnp
from jax import lax
from jax.sharding import PartitionSpec as P

LAT = 384
LON = 1024
MLAT = 96
MLON = 96


def lon_forward(first, count):
    index = first + jnp.arange(count, dtype=jnp.int32)
    modes = jnp.arange(MLON, dtype=jnp.int32)
    phase = index[:, None] * modes[None, :] % LON
    angle = phase.astype(jnp.float32) * (2.0 * math.pi / LON)
    scale = 1.0 / math.sqrt(LAT * LON)
    return (jnp.stack([jnp.cos(angle), -jnp.sin(angle)], 1) * scale).astype(jnp.bfloat16)


def lat_forward(first, count):
    freqs = jnp.arange(MLAT, dtype=jnp.int32) - MLAT // 2
    index = first + jnp.arange(count, dtype=jnp.int32)
    phase = jnp.mod(freqs[:, None] * index[None, :], LAT)
    angle = phase.astype(jnp.float32) * (2.0 * math.pi / LAT)
    cosine, sine = (jnp.cos(angle), jnp.sin(angle))
    return jnp.stack([jnp.stack([cosine, sine]), jnp.stack([-sine, cosine])])


def lat_inverse(first, count):
    freqs = jnp.arange(MLAT, dtype=jnp.int32) - MLAT // 2
    index = first + jnp.arange(count, dtype=jnp.int32)
    phase = jnp.mod(index[:, None] * freqs[None, :], LAT)
    angle = phase.astype(jnp.float32) * (2.0 * math.pi / LAT)
    cosine, sine = (jnp.cos(angle), jnp.sin(angle))
    return jnp.stack([jnp.stack([cosine, -sine]), jnp.stack([sine, cosine])]).astype(jnp.bfloat16)


def lon_inverse(first, count):
    modes = jnp.arange(MLON, dtype=jnp.int32)
    index = first + jnp.arange(count, dtype=jnp.int32)
    phase = modes[:, None] * index[None, :] % LON
    angle = phase.astype(jnp.float32) * (2.0 * math.pi / LON)
    factor = jnp.where(modes == 0, 1.0, 2.0).astype(jnp.float32)[:, None] / math.sqrt(LAT * LON)
    return jnp.stack([factor * jnp.cos(angle), -factor * jnp.sin(angle)]).astype(jnp.bfloat16)


def area_weights(first, count):
    index = first + jnp.arange(count, dtype=jnp.int32)
    return jnp.cos(math.pi * ((index.astype(jnp.float32) + 0.5) / LAT - 0.5))


def complex_block(pair):
    real_part, imag_part = (pair[0], pair[1])
    return jnp.stack(
        [jnp.stack([real_part, -imag_part], 1), jnp.stack([imag_part, real_part], 1)], 0
    )


def body(state, weights_in, bias_in, weights_out):
    batch, cdev, latdev, londev = state.shape
    nlat = lax.axis_size("lat")
    nlon = lax.axis_size("lon")
    lat_first = lax.axis_index("lat") * latdev
    lon_first = lax.axis_index("lon") * londev
    modes_lat = MLAT // nlat
    modes_lon = MLON // nlon
    qtab = lat_forward(lat_first, latdev)
    qsplit = qtab.reshape(2, 2, nlat, modes_lat, latdev)
    lonpart = jnp.einsum(
        "bcnl,lpk->pbcnk", state, lon_forward(lon_first, londev), preferred_element_type=jnp.float32
    )
    lonsplit = lonpart.reshape(2, batch, cdev, latdev, nlon, modes_lon)
    partial_value = jnp.einsum(
        "qpIJn,pbcnKk->qbcIKJk", qsplit, lonsplit, precision=lax.Precision.HIGHEST
    )
    spectrum = lax.psum_scatter(
        partial_value.reshape(2, batch, cdev, -1), ("lat", "lon"), scatter_dimension=3, tiled=True
    )
    spectrum = spectrum.astype(jnp.bfloat16)
    block_in = complex_block(weights_in)
    block_out = complex_block(weights_out)
    whole = lax.all_gather(spectrum, "var", axis=2, tiled=True)
    owned = lax.dynamic_slice_in_dim(block_out, lax.axis_index("var") * cdev, cdev, 1)
    hidden = jnp.einsum("qhpc,pbcj->qbhj", block_in, whole, preferred_element_type=jnp.float32)
    hidden = jnp.maximum(hidden + bias_in[:, None, :, None], 0.0).astype(jnp.bfloat16)
    mixed = jnp.einsum("qoph,pbhj->qboj", owned, hidden, preferred_element_type=jnp.float32).astype(
        jnp.bfloat16
    )
    mixed = mixed.reshape(2, batch, cdev, modes_lat, modes_lon)
    rtab = lat_inverse(lat_first, latdev)
    table = rtab
    latback = jnp.einsum(
        "qpnj,pbcjk->qbcnk",
        table,
        lax.all_gather(mixed, "lat", axis=3, tiled=True),
        preferred_element_type=jnp.float32,
    ).astype(jnp.bfloat16)
    htab = lon_inverse(lon_first, londev)
    table = htab
    result = jnp.einsum(
        "pbcnk,pkl->bcnl",
        lax.all_gather(latback, "lon", axis=4, tiled=True),
        table,
        preferred_element_type=jnp.float32,
    )
    active = jax.nn.gelu(result, approximate=False)
    field = active.astype(jnp.bfloat16)
    weights = area_weights(lat_first, latdev)
    denominator = batch * LON * jnp.sum(area_weights(0, LAT))
    row_total = jnp.sum(active, -1)
    row_square = jnp.sum(active * active, -1)
    summed, squared = lax.psum((row_total, row_square), "lon")
    zonal = summed / LON
    local = jnp.sum(squared * weights[None, None, :], axis=(0, 2))
    energy = lax.psum(local, "lat") / denominator
    return (field, zonal, energy)


def solution(mesh):
    return jax.shard_map(
        body,
        mesh=mesh,
        in_specs=(P(None, "var", "lat", "lon"), P(), P(), P()),
        out_specs=(P(None, "var", "lat", "lon"), P(None, "var", "lat"), P("var")),
        check_vma=False,
    )
```

profile of v0, /device:TPU:0, one launch (start us, length us, event | category | flops | bytes accessed | tf_op | source)
XLA Modules:
  0.0 286.0 jit_solution(11124718657220605227)
XLA Ops:
  7.2 0.8 fusion.71
  8.1 0.3 fusion.82
  8.3 4.4 %fusion.15 = f32[2,96,64,96]{3,1,2,0:T(8,128)S(1)} fusion(bf16[1,64,96,512]{3,2,1,0:T(8,128)(2,1)} %param.4, f32[512,1,96]{0,2,1:T(8,128)S(1)} %get-tuple-element.24, f32[512,1,96]{0,2,1:T(8,128)S(1)} %get-tuple-element.23), kind=kOutput, calls=%fused_computation.25 | convolution fusion | flops 1208254464 | bytes 11403264 | tf_op jit(solution)/shard_map/bcnl,lpk->pbcnk/dot_general | solution.py:71
  12.8 12.8 %fusion.17 = f32[2,1,64,4,2,24,48]{2,5,3,0,6,4,1:T(8,128)} fusion(f32[2,64,96,2,48,1,1]{2,4,3,1,0,6,5:T(8,128)S(1)} %bitcast.169, f32[1,1,4,24,96]{4,3,1,2,0:T(8,128)S(1)} %get-tuple-element.20, f32[1,1,4,24,96]{4,3,1,2,0:T(8,128)S(1)} %get-tuple-element.19, f32[1,1,4,24,96]{4,3,1,2,0:T(8,128)S(1)} %get-tuple-element.18), kind=kOutput, calls=%fused_computation.28 | convolution fusion | flops 2718019584 | bytes 9547776 | tf_op jit(solution)/shard_map/qpIJn,pbcnKk->qbcIKJk/dot_general | solution.py:75
  25.6 12.4 %copy.27 = f32[2,1,64,4,2,24,48]{6,5,4,3,2,0,1:T(8,128)} copy(f32[2,1,64,4,2,24,48]{2,5,3,0,6,4,1:T(8,128)} %fusion.17) | data formatting | bytes 9437184 | tf_op jit(solution)/shard_map/qpIJn,pbcnKk->qbcIKJk/transpose | solution.py:75
  38.0 13.1 %reshape.714 = f32[2,1,64,9216]{3,2,0,1:T(8,128)} reshape(f32[2,1,64,4,2,24,48]{6,5,4,3,2,0,1:T(8,128)} %copy.27) | data formatting | bytes 9437184 | tf_op jit(solution)/shard_map/reshape | solution.py:79
  51.1 0.0 all-gather.4.cloned.1.call-start
  51.2 56.6 %reduce-scatter.2.cloned.1.call-done = f32[2,1,64,1152]{3,2,0,1:T(8,128)} async-done(((f32[2,1,64,9216]{3,2,0,1:T(8,128)}), f32[2,1,64,1152]{3,2,0,1:T(8,128)}) %reduce-scatter.2.cloned.1.call-update) | async-done | bytes 589840 | tf_op jit(solution)/shard_map/reduce_scatter | solution.py:78
  107.8 1.1 convert_element_type.119
  108.9 1.0 copy.28
  109.9 0.2 all-gather.6.cloned.1.call-start
  110.3 0.1 maximum_bitcast_fusion
  110.4 30.0 %all-gather.4.cloned.1.call-done = bf16[2,1,256,1152]{3,0,1,2:T(2,128)(2,1)} async-done(((bf16[2,1,64,1152]{3,0,1,2:T(2,128)(2,1)}), bf16[2,1,256,1152]{3,0,1,2:T(2,128)(2,1)}) %all-gather.4.cloned.1.call-update) | async-done | bytes 1179664 | tf_op jit(solution)/shard_map/all_gather | solution.py:84
  140.3 3.5 %copy.29 = bf16[2,1,256,1152]{2,3,0,1:T(8,128)(2,1)S(1)} copy(bf16[2,1,256,1152]{3,0,1,2:T(2,128)(2,1)} %all-gather.4.cloned.1.call-done) | data formatting | bytes 2359296 | tf_op jit(solution)/shard_map/all_gather | solution.py:84
  143.8 1.1 fusion.28
  144.9 0.7 reshape.717
  145.7 1.3 copy.31
  147.0 0.0 all-gather.8.cloned.1.call-start
  147.1 0.3 negate_convert_fusion
  147.4 23.0 %all-gather.6.cloned.1.call-done = bf16[2,1,64,96,48]{2,4,1,0,3:T(8,128)(2,1)} async-done(((bf16[2,1,64,24,48]{2,4,1,0,3:T(8,128)(2,1)}), bf16[2,1,64,96,48]{2,4,1,0,3:T(8,128)(2,1)}) %all-gather.6.cloned.1.call-update) | async-done | bytes 1179664 | tf_op jit(solution)/shard_map/all_gather | solution.py:97
  170.4 4.4 %fusion.31 = bf16[2,1,64,96,48]{3,2,1,0,4:T(8,128)(2,1)} fusion(bf16[2,64,96,48,1]{1,3,0,2,4:T(8,128)(2,1)} %bitcast.170, bf16[1,2,96,96]{3,2,1,0:T(8,128)(2,1)S(1)} %get-tuple-element.17, bf16[1,2,96,96]{3,2,1,0:T(8,128)(2,1)S(1)} %get-tuple-element.16), kind=kOutput, calls=%fused_computation.41 | convolution fusion | flops 227229696 | bytes 2433024 | tf_op jit(solution)/shard_map/qpnj,pbcjk->qbcnk/dot_general | solution.py:94
  174.9 0.6 cosine_reduce_fusion
  176.2 0.1 multiply_cosine_fusion
  176.2 0.8 multiply_convert_fusion.1
  177.0 42.9 %all-gather.8.cloned.1.call-done = bf16[2,1,64,96,96]{3,2,1,0,4:T(8,128)(2,1)} async-done(((bf16[2,1,64,96,48]{3,2,1,0,4:T(8,128)(2,1)}), bf16[2,1,64,96,96]{3,2,1,0,4:T(8,128)(2,1)}) %all-gather.8.cloned.1.call-update) | async-done | bytes 2359312 | tf_op jit(solution)/shard_map/all_gather | solution.py:104
  219.9 4.8 %copy.34 = bf16[2,1,64,96,96]{4,3,0,2,1:T(8,128)(2,1)S(1)} copy(bf16[2,1,64,96,96]{3,2,1,0,4:T(8,128)(2,1)} %all-gather.8.cloned.1.call-done) | data formatting | bytes 4718592 | tf_op jit(solution)/shard_map/all_gather | solution.py:104
  224.7 40.1 %multiply_reduce_fusion = (f32[64,96]{1,0:T(8,128)S(1)}, f32[64,96]{1,0:T(8,128)S(1)}, bf16[1,64,96,512]{3,2,1,0:T(8,128)(2,1)}) fusion(bf16[1,96,512]{2,1,0:T(8,128)(2,1)S(1)} %get-tuple-element.22, bf16[1,96,512]{2,1,0:T(8,128)(2,1)S(1)} %get-tuple-element.21, bf16[2,1,64,96,96]{4,3,0,2,1:T(8,128)(2,1)S(1)} %copy.34), kind=kOutput, calls=%fused_computation.6 | convolution fusion | flops 1421955072 | bytes 8896512 | tf_op jit(solution)/shard_map/pbcnk,pkl->bcnl/dot_general | solution.py:102
  264.9 7.7 %all-reduce = (f32[1,64,96]{2,1,0:T(8,128)S(1)}, f32[1,64,96]{2,1,0:T(8,128)S(1)}) all-reduce(f32[1,64,96]{2,1,0:T(8,128)S(1)} %bitcast.172, f32[1,64,96]{2,1,0:T(8,128)S(1)} %bitcast.171), channel_id=1, replica_groups=mesh['var'=4,'lat'=4,'lon'=2] {'lon'}, use_global_device_ids=true, to_apply=%region_2.3 | all-reduce | flops 12288 | bytes 98304 | tf_op jit(solution)/shard_map/psum | solution.py:114
  272.5 0.6 broadcast_multiply_fusion
  273.2 0.1 multiply_reduce_fusion.1
  273.3 5.7 %psum.23 = f32[64]{0:T(128)S(1)} all-reduce(f32[64]{0:T(128)S(1)} %multiply_reduce_fusion.1), channel_id=1, replica_groups=mesh['var'=4,'lat'=4,'lon'=2] {'lat'}, use_global_device_ids=true, to_apply=%region_6.7 | all-reduce | flops 64 | bytes 512 | tf_op jit(solution)/shard_map/psum | solution.py:117
  278.9 0.5 broadcast_divide_fusion
  (20 shorter events, 0.2 us)
Async XLA Ops:
  7.2 100.6 %reduce-scatter.2.cloned.1.call-start = ((), (), s32[]{:S(2)}) async-start(), calls=%async_computation.1 | async-start | bytes 5308416 | tf_op jit(solution)/shard_map/reduce_scatter | solution.py:78
  38.0 72.2 %copy-start = (bf16[2,256,256]{2,1,0:T(8,128)(2,1)S(1)}, bf16[2,256,256]{2,1,0:T(8,128)(2,1)}, u32[]{:S(2)}) copy-start(bf16[2,256,256]{2,1,0:T(8,128)(2,1)} %param.5) | copy-start | bytes 786436
  38.0 72.2 %copy-start.1 = (bf16[2,256,256]{2,1,0:T(8,128)(2,1)S(1)}, bf16[2,256,256]{2,1,0:T(8,128)(2,1)}, u32[]{:S(2)}) copy-start(bf16[2,256,256]{2,1,0:T(8,128)(2,1)} %param.7) | copy-start | bytes 786436
  38.0 105.8 %copy-start.2 = (f32[2,256]{1,0:T(2,128)S(1)}, f32[2,256]{1,0:T(2,128)}, u32[]{:S(2)}) copy-start(f32[2,256]{1,0:T(2,128)} %param.6) | copy-start | bytes 6148
  51.1 89.2 %all-gather.4.cloned.1.call-start = ((), (), s32[]{:S(2)}) async-start(), calls=%async_computation.2 | async-start | bytes 1474560 | tf_op jit(solution)/shard_map/all_gather | solution.py:84
  109.9 60.5 %all-gather.6.cloned.1.call-start = ((), (), s32[]{:S(2)}) async-start(), calls=%async_computation.3 | async-start | bytes 2949120 | tf_op jit(solution)/shard_map/all_gather | solution.py:97
  147.0 72.9 %all-gather.8.cloned.1.call-start = ((), (), s32[]{:S(2)}) async-start(), calls=%async_computation.4 | async-start | bytes 4718592 | tf_op jit(solution)/shard_map/all_gather | solution.py:104
Sparse Core Ops, SparseCore 0:
  51.2 56.4 reduce-scatter.1
  110.0 30.2 all-gather.3
  147.1 23.2 all-gather.5
  175.0 44.9 all-gather.7
where the time goes:
time: 287 us; the launch traced here: 286 us
  waiting for transfers between devices  153 us (53%)
  matrix products  62.9 us (22%)
  local copies, waits for them, and re-layouts  36.8 us (13%)
  between operations  14.6 us (5%)
  blocking collectives  13.3 us (5%)
  other arithmetic  5.38 us (2%)
    reduce_scatter x1, waiting for transfers between devices, body(): lax.psum_scatter(partial_value.reshape(2, batch, cdev, -1), ('lat', 'lon'...  56.6 us
    all_gather x1, waiting for transfers between devices, body(): lax.all_gather(latback, 'lon', axis=4, tiled=True)  42.9 us
    dot_general x1, matrix products, body(): jnp.einsum('pbcnk,pkl->bcnl', lax.all_gather(latback, 'lon', axis=4, tile...  40.1 us
    all_gather x1, waiting for transfers between devices, body(): whole = lax.all_gather(spectrum, 'var', axis=2, tiled=True)  30 us
    all_gather x1, waiting for transfers between devices, body(): lax.all_gather(mixed, 'lat', axis=3, tiled=True)  23 us
    reshape x1, local copies, waits for them, and re-layouts, body(): partial_value.reshape(2, batch, cdev, -1)  13.1 us
    dot_general x1, matrix products, body(): jnp.einsum('qpIJn,pbcnKk->qbcIKJk', qsplit, lonsplit, precision=lax.Preci...  12.8 us
    transpose x1, local copies, waits for them, and re-layouts, body(): jnp.einsum('qpIJn,pbcnKk->qbcIKJk', qsplit, lonsplit, precision=lax.Preci...  12.4 us
  transfers between devices with their start and end apart: 4, of which 4 were waited for; matrix products, arithmetic and copies ran while one was open for 1% of the time, Pallas kernels for 0%

commit v1 on v0

--- a/solution.py
+++ b/solution.py
@@ -8,6 +8,17 @@
 LON = 1024
 MLAT = 96
 MLON = 96
+
+
+def pass_along(shard, axis, dim):
+    count = lax.axis_size(axis)
+    right = [(i, (i + 1) % count) for i in range(count)]
+    parts = [shard]
+    for stride in range(1, count):
+        parts = [lax.ppermute(parts[0], axis, right), *parts]
+    whole = jnp.concatenate(parts, axis=dim)
+    places = (lax.axis_index(axis) + 1) * parts[-1].shape[dim]
+    return jnp.roll(whole, places, axis=dim)
 
 
 def lon_forward(first, count):
@@ -81,7 +92,7 @@
     spectrum = spectrum.astype(jnp.bfloat16)
     block_in = complex_block(weights_in)
     block_out = complex_block(weights_out)
-    whole = lax.all_gather(spectrum, "var", axis=2, tiled=True)
+    whole = pass_along(spectrum, "var", 2)
     owned = lax.dynamic_slice_in_dim(block_out, lax.axis_index("var") * cdev, cdev, 1)
     hidden = jnp.einsum("qhpc,pbcj->qbhj", block_in, whole, preferred_element_type=jnp.float32)
     hidden = jnp.maximum(hidden + bias_in[:, None, :, None], 0.0).astype(jnp.bfloat16)

time: 287 us -> 284 us (0.990)
  waiting for transfers between devices: 153 us -> 147 us
  local copies, waits for them, and re-layouts: 36.8 us -> 33.9 us
    all_gather x1 -> x0, waiting for transfers between devices: 30 us -> none  [body(): whole = lax.all_gather(spectrum, 'var', axis=2, tiled=True)]
    ppermute x0 -> x3, waiting for transfers between devices: none -> 26.9 us  [pass_along(): parts = [lax.ppermute(parts[0], axis, right), *parts]]
    all_gather x1 -> x0, local copies, waits for them, and re-layouts: 3.45 us -> none  [body(): whole = lax.all_gather(spectrum, 'var', axis=2, tiled=True)]
  transfers between devices with their start and end apart: 4 -> 6, of which waited for: 4 -> 6; matrix products, arithmetic and copies ran while one was open for 1% -> 1% of each run, Pallas kernels for 0% -> 0%
where the time goes in v1:
time: 284 us; the launch traced here: 283 us
  waiting for transfers between devices  147 us (52%)
  matrix products  64.2 us (23%)
  local copies, waits for them, and re-layouts  33.9 us (12%)
  between operations  14.6 us (5%)
  blocking collectives  13.3 us (5%)
  other arithmetic  7.59 us (3%)
    reduce_scatter x1, waiting for transfers between devices, body(): lax.psum_scatter(partial_value.reshape(2, batch, cdev, -1), ('lat', 'lon'...  56.6 us
    all_gather x1, waiting for transfers between devices, body(): lax.all_gather(latback, 'lon', axis=4, tiled=True)  42.9 us
    dot_general x1, matrix products, body(): jnp.einsum('pbcnk,pkl->bcnl', lax.all_gather(latback, 'lon', axis=4, tile...  40.1 us
    ppermute x3, waiting for transfers between devices, pass_along(): parts = [lax.ppermute(parts[0], axis, right), *parts]  26.9 us
    all_gather x1, waiting for transfers between devices, body(): lax.all_gather(mixed, 'lat', axis=3, tiled=True)  21 us
    reshape x1, local copies, waits for them, and re-layouts, body(): partial_value.reshape(2, batch, cdev, -1)  13.1 us
    dot_general x1, matrix products, body(): jnp.einsum('qpIJn,pbcnKk->qbcIKJk', qsplit, lonsplit, precision=lax.Preci...  12.8 us
    transpose x1, local copies, waits for them, and re-layouts, body(): jnp.einsum('qpIJn,pbcnKk->qbcIKJk', qsplit, lonsplit, precision=lax.Preci...  12.3 us
  transfers between devices with their start and end apart: 6, of which 6 were waited for; matrix products, arithmetic and copies ran while one was open for 1% of the time, Pallas kernels for 0%

profile of v1, /device:TPU:0, one launch (start us, length us, event | category | flops | bytes accessed | tf_op | source)
XLA Modules:
  0.0 282.8 jit_solution(7830496611080861767)
XLA Ops:
  7.2 0.8 fusion.72
  8.1 0.3 fusion.83
  8.3 4.4 %fusion.15 = f32[2,96,64,96]{3,1,2,0:T(8,128)S(1)} fusion(bf16[1,64,96,512]{3,2,1,0:T(8,128)(2,1)} %param.4, f32[512,1,96]{0,2,1:T(8,128)S(1)} %get-tuple-element.24, f32[512,1,96]{0,2,1:T(8,128)S(1)} %get-tuple-element.23), kind=kOutput, calls=%fused_computation.25 | convolution fusion | flops 1208254464 | bytes 11403264 | tf_op jit(solution)/shard_map/bcnl,lpk->pbcnk/dot_general | solution.py:82
  12.8 12.8 %fusion.17 = f32[2,1,64,4,2,24,48]{2,5,3,0,6,4,1:T(8,128)} fusion(f32[2,64,96,2,48,1,1]{2,4,3,1,0,6,5:T(8,128)S(1)} %bitcast.170, f32[1,1,4,24,96]{4,3,1,2,0:T(8,128)S(1)} %get-tuple-element.20, f32[1,1,4,24,96]{4,3,1,2,0:T(8,128)S(1)} %get-tuple-element.19, f32[1,1,4,24,96]{4,3,1,2,0:T(8,128)S(1)} %get-tuple-element.18), kind=kOutput, calls=%fused_computation.28 | convolution fusion | flops 2718019584 | bytes 9547776 | tf_op jit(solution)/shard_map/qpIJn,pbcnKk->qbcIKJk/dot_general | solution.py:86
  25.6 12.3 %copy.26 = f32[2,1,64,4,2,24,48]{6,5,4,3,2,0,1:T(8,128)} copy(f32[2,1,64,4,2,24,48]{2,5,3,0,6,4,1:T(8,128)} %fusion.17) | data formatting | bytes 9437184 | tf_op jit(solution)/shard_map/qpIJn,pbcnKk->qbcIKJk/transpose | solution.py:86
  38.0 13.1 %reshape.714 = f32[2,1,64,9216]{3,2,0,1:T(8,128)} reshape(f32[2,1,64,4,2,24,48]{6,5,4,3,2,0,1:T(8,128)} %copy.26) | data formatting | bytes 9437184 | tf_op jit(solution)/shard_map/reshape | solution.py:90
  51.2 56.6 %reduce-scatter.2.cloned.1.call-done = f32[2,1,64,1152]{3,2,0,1:T(8,128)} async-done(((f32[2,1,64,9216]{3,2,0,1:T(8,128)}), f32[2,1,64,1152]{3,2,0,1:T(8,128)}) %reduce-scatter.2.cloned.1.call-update) | async-done | bytes 589840 | tf_op jit(solution)/shard_map/reduce_scatter | solution.py:89
  107.7 1.1 convert_element_type.119
  108.8 1.5 collective-permute-start
  110.4 8.9 %collective-permute-done = bf16[2,1,64,1152]{3,2,0,1:T(8,128)(2,1)S(1)} collective-permute-done((bf16[2,1,64,1152]{3,2,0,1:T(8,128)(2,1)S(1)}, bf16[2,1,64,1152]{3,2,0,1:T(8,128)(2,1)S(1)}, u32[]{:S(2)}, u32[]{:S(2)}) %collective-permute-start) | collective-permute-done | bytes 294944 | tf_op jit(solution)/shard_map/ppermute | solution.py:18
  119.4 9.5 %collective-permute-done.1 = bf16[2,1,64,1152]{3,2,0,1:T(8,128)(2,1)S(1)} collective-permute-done((bf16[2,1,64,1152]{3,2,0,1:T(8,128)(2,1)S(1)}, bf16[2,1,64,1152]{3,2,0,1:T(8,128)(2,1)S(1)}, u32[]{:S(2)}, u32[]{:S(2)}) %collective-permute-start.1) | collective-permute-done | bytes 294944 | tf_op jit(solution)/shard_map/ppermute | solution.py:18
  128.9 0.1 maximum_bitcast_fusion
  129.0 8.6 %collective-permute-done.2 = bf16[2,1,64,1152]{3,2,0,1:T(8,128)(2,1)S(1)} collective-permute-done((bf16[2,1,64,1152]{3,2,0,1:T(8,128)(2,1)S(1)}, bf16[2,1,64,1152]{3,2,0,1:T(8,128)(2,1)S(1)}, u32[]{:S(2)}, u32[]{:S(2)}) %collective-permute-start.2) | collective-permute-done | bytes 294944 | tf_op jit(solution)/shard_map/ppermute | solution.py:18
  137.6 1.1 constant_dynamic-update-slice_fusion.4
  138.8 1.1 constant_dynamic-update-slice_fusion
  140.0 1.4 copy-done.2
  141.4 2.4 fusion.28
  143.8 0.7 reshape.717
  144.5 1.3 copy.29
  145.9 0.3 negate_convert_fusion
  146.2 21.0 %all-gather.3.cloned.1.call-done = bf16[2,1,64,96,48]{2,4,1,0,3:T(8,128)(2,1)} async-done(((bf16[2,1,64,24,48]{2,4,1,0,3:T(8,128)(2,1)}), bf16[2,1,64,96,48]{2,4,1,0,3:T(8,128)(2,1)}) %all-gather.3.cloned.1.call-update) | async-done | bytes 1179664 | tf_op jit(solution)/shard_map/all_gather | solution.py:108
  167.3 4.4 %fusion.31 = bf16[2,1,64,96,48]{3,2,1,0,4:T(8,128)(2,1)} fusion(bf16[2,64,96,48,1]{1,3,0,2,4:T(8,128)(2,1)} %bitcast.171, bf16[1,2,96,96]{3,2,1,0:T(8,128)(2,1)S(1)} %get-tuple-element.17, bf16[1,2,96,96]{3,2,1,0:T(8,128)(2,1)S(1)} %get-tuple-element.16), kind=kOutput, calls=%fused_computation.41 | convolution fusion | flops 227229696 | bytes 2433024 | tf_op jit(solution)/shard_map/qpnj,pbcjk->qbcnk/dot_general | solution.py:105
  171.7 0.6 cosine_reduce_fusion
  173.0 0.8 multiply_convert_fusion.1
  173.9 42.9 %all-gather.5.cloned.1.call-done = bf16[2,1,64,96,96]{3,2,1,0,4:T(8,128)(2,1)} async-done(((bf16[2,1,64,96,48]{3,2,1,0,4:T(8,128)(2,1)}), bf16[2,1,64,96,96]{3,2,1,0,4:T(8,128)(2,1)}) %all-gather.5.cloned.1.call-update) | async-done | bytes 2359312 | tf_op jit(solution)/shard_map/all_gather | solution.py:115
  216.7 4.8 %copy.32 = bf16[2,1,64,96,96]{4,3,0,2,1:T(8,128)(2,1)S(1)} copy(bf16[2,1,64,96,96]{3,2,1,0,4:T(8,128)(2,1)} %all-gather.5.cloned.1.call-done) | data formatting | bytes 4718592 | tf_op jit(solution)/shard_map/all_gather | solution.py:115
  221.5 40.1 %multiply_reduce_fusion = (f32[64,96]{1,0:T(8,128)S(1)}, f32[64,96]{1,0:T(8,128)S(1)}, bf16[1,64,96,512]{3,2,1,0:T(8,128)(2,1)}) fusion(bf16[1,96,512]{2,1,0:T(8,128)(2,1)S(1)} %get-tuple-element.22, bf16[1,96,512]{2,1,0:T(8,128)(2,1)S(1)} %get-tuple-element.21, bf16[2,1,64,96,96]{4,3,0,2,1:T(8,128)(2,1)S(1)} %copy.32), kind=kOutput, calls=%fused_computation.6 | convolution fusion | flops 1421955072 | bytes 8896512 | tf_op jit(solution)/shard_map/pbcnk,pkl->bcnl/dot_general | solution.py:113
  261.7 7.7 %all-reduce = (f32[1,64,96]{2,1,0:T(8,128)S(1)}, f32[1,64,96]{2,1,0:T(8,128)S(1)}) all-reduce(f32[1,64,96]{2,1,0:T(8,128)S(1)} %bitcast.173, f32[1,64,96]{2,1,0:T(8,128)S(1)} %bitcast.172), channel_id=1, replica_groups=mesh['var'=4,'lat'=4,'lon'=2] {'lon'}, use_global_device_ids=true, to_apply=%region_2.3 | all-reduce | flops 12288 | bytes 98304 | tf_op jit(solution)/shard_map/psum | solution.py:125
  269.4 0.6 broadcast_multiply_fusion
  270.0 0.1 multiply_reduce_fusion.1
  270.1 5.7 %psum.23 = f32[64]{0:T(128)S(1)} all-reduce(f32[64]{0:T(128)S(1)} %multiply_reduce_fusion.1), channel_id=1, replica_groups=mesh['var'=4,'lat'=4,'lon'=2] {'lat'}, use_global_device_ids=true, to_apply=%region_6.7 | all-reduce | flops 64 | bytes 512 | tf_op jit(solution)/shard_map/psum | solution.py:128
  275.7 0.5 broadcast_divide_fusion
  (31 shorter events, 0.5 us)
Async XLA Ops:
  7.2 100.6 %reduce-scatter.2.cloned.1.call-start = ((), (), s32[]{:S(2)}) async-start(), calls=%async_computation.1 | async-start | bytes 5308416 | tf_op jit(solution)/shard_map/reduce_scatter | solution.py:89
  37.9 72.4 %copy-start = (bf16[2,256,256]{2,1,0:T(8,128)(2,1)S(1)}, bf16[2,256,256]{2,1,0:T(8,128)(2,1)}, u32[]{:S(2)}) copy-start(bf16[2,256,256]{2,1,0:T(8,128)(2,1)} %param.5) | copy-start | bytes 786436
  38.0 81.4 %copy-start.1 = (bf16[2,256,256]{2,1,0:T(8,128)(2,1)S(1)}, bf16[2,256,256]{2,1,0:T(8,128)(2,1)}, u32[]{:S(2)}) copy-start(bf16[2,256,256]{2,1,0:T(8,128)(2,1)} %param.7) | copy-start | bytes 786436
  38.0 103.4 %copy-start.3 = (f32[2,256]{1,0:T(2,128)S(1)}, f32[2,256]{1,0:T(2,128)}, u32[]{:S(2)}) copy-start(f32[2,256]{1,0:T(2,128)} %param.6) | copy-start | bytes 6148
  51.1 116.2 %all-gather.3.cloned.1.call-start = ((), (), s32[]{:S(2)}) async-start(), calls=%async_computation.2 | async-start | bytes 2949120 | tf_op jit(solution)/shard_map/all_gather | solution.py:108
  108.8 10.4 %collective-permute-start = (bf16[2,1,64,1152]{3,2,0,1:T(8,128)(2,1)S(1)}, bf16[2,1,64,1152]{3,2,0,1:T(8,128)(2,1)S(1)}, u32[]{:S(2)}, u32[]{:S(2)}) collective-permute-start(bf16[2,1,64,1152]{3,2,0,1:T(8,128)(2,1)S(1)} %convert_element_type.119), channel_id=1, source_target_pairs={{0,8},{8,16},{16,24},{24,0},{1,9},{9,17},{17,25},{25,1},{2,10},{10... | collective-permute-start | bytes 884744 | tf_op jit(solution)/shard_map/ppermute | solution.py:18
  119.3 9.5 %collective-permute-start.1 = (bf16[2,1,64,1152]{3,2,0,1:T(8,128)(2,1)S(1)}, bf16[2,1,64,1152]{3,2,0,1:T(8,128)(2,1)S(1)}, u32[]{:S(2)}, u32[]{:S(2)}) collective-permute-start(bf16[2,1,64,1152]{3,2,0,1:T(8,128)(2,1)S(1)} %collective-permute-done), channel_id=1, source_target_pairs={{0,8},{8,16},{16,24},{24,0},{1,9},{9,17},{17,25},{25,1},{2,10},{10... | collective-permute-start | bytes 884744 | tf_op jit(solution)/shard_map/ppermute | solution.py:18
  128.8 8.7 %collective-permute-start.2 = (bf16[2,1,64,1152]{3,2,0,1:T(8,128)(2,1)S(1)}, bf16[2,1,64,1152]{3,2,0,1:T(8,128)(2,1)S(1)}, u32[]{:S(2)}, u32[]{:S(2)}) collective-permute-start(bf16[2,1,64,1152]{3,2,0,1:T(8,128)(2,1)S(1)} %collective-permute-done.1), channel_id=1, source_target_pairs={{0,8},{8,16},{16,24},{24,0},{1,9},{9,17},{17,25},{25,1},{2,10},{10... | collective-permute-start | bytes 884744 | tf_op jit(solution)/shard_map/ppermute | solution.py:18
  140.0 1.4 copy-start.2
  145.9 70.9 %all-gather.5.cloned.1.call-start = ((), (), s32[]{:S(2)}) async-start(), calls=%async_computation.3 | async-start | bytes 4718592 | tf_op jit(solution)/shard_map/all_gather | solution.py:115
Sparse Core Ops, SparseCore 0:
  51.2 56.4 reduce-scatter.1
  146.0 21.2 all-gather.2
  171.8 44.9 all-gather.4
